TPU v7x, 32 devices: a whole 2x2x4 slice. The times are simulated.
32 devices in a mesh: member: 2 (over x), gx: 8 (over z, y), gy: 2 (over core).
Axes of the slice: x: 2, y: 2, z: 4, core: 2. Of those that a mesh axis runs over, the one named last changes fastest.
Arguments:
- conc: float32 [66, 4, 64, 256], P(None, None, ('member', 'gx'), 'gy'), parts along dimension 2, may hold values from 0.001 to 30
- winds: float32 [2, 4, 64, 256], P(None, None, ('member', 'gx'), 'gy'), parts along dimension 2, may hold values from -0.9 to 0.9
- diffusivity: float32 [3, 64, 256], P(None, ('member', 'gx'), 'gy'), parts along dimension 1, may hold values from 0.1 to 10
- emission: float32 [66, 64, 256], P(None, ('member', 'gx'), 'gy'), parts along dimension 1, may hold values from 0.1 to 1
- photo_rate: float32 [66], replicated, may hold values from 0.05 to 1
Outputs:
- conc_next: float32 [66, 4, 64, 256], P(None, None, ('member', 'gx'), 'gy'), parts along dimension 2
There are 2 independent parts, one for each index of `member`. A program takes and returns all parts, laid end to end along the dimension named above; an argument that names none is the same for every part. Nothing has to cross between parts.
All inputs are finite; a program needn't handle non-finite values.
Results may differ from a plain program's by a relative error of at most 0.00002.
Values sent between devices are 32-bit elements; how exact they have to be, the bound alone decides.
A program may use at most 64 MiB of HBM per device.

v0:
```python
import functools

import jax
import jax.numpy as jnp
from jax import lax
from jax.experimental import pallas as pl
from jax.experimental.pallas import tpu as pltpu
from jax.sharding import PartitionSpec as P

BETAS = (1.0 / 3.0, 0.5, 1.0)
SUB = 8
LANES = 128
PAD = 3
CHUNKS = 3


def stencil_weights(km, kp):
    def face(k):
        k = k / 60.0
        a = jnp.abs(k)
        return (
            k + a,
            -8.0 * k - 5.0 * a,
            37.0 * k + 10.0 * a,
            37.0 * k - 10.0 * a,
            -8.0 * k + 5.0 * a,
            k - a,
        )

    m, p = face(km), face(kp)
    return [-m[0]] + [p[j] - m[j + 1] for j in range(5)] + [p[5]]


def kernel(dims, conc_hbm, wind_hbm, diff_hbm, emis_hbm, rate_ref, out_hbm,
           conc_ref, wind_ref, diff_ref, emis_ref,
           send, state0, state_a, state_b, result, back, wsend, wrecv, cbuf, wx, wy,
           stat, stats, prate, coef,
           load_sem, in_send, in_recv, w_send, w_recv, h_send, h_recv,
           out_send, out_recv, s_send, s_recv, out_ref, store_sem):
    spec, lev, rows, halves, gx_n, span, tiles, chunks = dims
    n = gx_n * halves
    width = tiles // chunks
    deep = span * rows
    crews = gx_n // span
    my_gx, my_gy = lax.axis_index("gx"), lax.axis_index("gy")
    me = my_gx * halves + my_gy
    crew, seat = my_gx // span, my_gx % span
    my_lev = seat * halves + my_gy
    has_down, has_up = crew > 0, crew < crews - 1

    def where_is(dev):
        return {"gx": dev // halves, "gy": dev % halves}

    barrier = pltpu.get_barrier_semaphore()

    def greet(k, carry):
        pl.semaphore_signal(barrier, inc=1, device_id=where_is((me + k) % n),
                            device_id_type=pl.DeviceIdType.MESH)
        return carry

    lax.fori_loop(1, n, greet, 0)
    loads = [pltpu.make_async_copy(src, dst, load_sem.at[i]) for i, (src, dst) in enumerate(
        ((wind_hbm, wind_ref), (conc_hbm, conc_ref), (diff_hbm, diff_ref), (emis_hbm, emis_ref)))]
    for load in loads:
        load.start()

    stride = lev * rows
    loads[0].wait()
    for lv in range(lev):
        wsend[lv, 0:rows, :] = wind_ref[pl.ds(lv * rows, rows), :]
        wsend[lv, rows:2 * rows, :] = wind_ref[pl.ds((lev + lv) * rows, rows), :]
    loads[1].wait()
    for t in range(tiles):
        have = max(0, min(SUB, spec - t * SUB))
        for lv in range(lev):
            for r in range(rows):
                if have < SUB:
                    send[lv, t, r, :, :] = jnp.zeros((SUB, LANES), jnp.float32)
                if have > 0:
                    send[lv, t, r, 0:have, :] = conc_ref[
                        pl.ds(t * SUB * stride + lv * rows + r, have, stride=stride), :]

    pl.semaphore_wait(barrier, n - 1)

    def remote(src, dst, dev, s_sem, r_sem):
        return pltpu.make_async_remote_copy(
            src_ref=src, dst_ref=dst, send_sem=s_sem, recv_sem=r_sem,
            device_id=where_is(dev), device_id_type=pl.DeviceIdType.MESH)

    def deliver(src, dst, dev, s_sem, r_sem):
        @pl.when(dev == me)
        def _():
            pltpu.make_async_copy(src, dst, r_sem).start()

        @pl.when(dev != me)
        def _():
            remote(src, dst, dev, s_sem, r_sem).start()

    def sent(src, s_sem):
        pltpu.make_async_copy(src, src, s_sem).wait()

    def landed(dst, r_sem):
        pltpu.make_async_copy(dst, dst, r_sem).wait()

    def mate(lv):
        return (crew * span + lv // halves) * halves + lv % halves

    def tile_range(c):
        return pl.ds(c * width, width)

    sides = ((0, None, None), (1, has_up & (seat == span - 1), 0),
             (-1, has_down & (seat == 0), span + 1))

    def for_winds(act):
        for o, (shift, cond, slot) in enumerate(sides):
            at = seat + 1 if slot is None else slot
            for lv in range(lev):
                dev = mate(lv) + shift * span * halves
                if cond is None:
                    act(o, lv, dev, at)
                else:
                    pl.when(cond)(functools.partial(act, o, lv, dev, at))

    for_winds(lambda o, lv, dev, at: deliver(
        wsend.at[lv], wrecv.at[at * halves + my_gy], dev, w_send.at[o, lv],
        w_recv.at[at * halves + my_gy]))
    for c in range(chunks):
        for lv in range(lev):
            deliver(send.at[lv, tile_range(c)],
                    state0.at[tile_range(c), my_gy, pl.ds(PAD + seat * rows, rows)],
                    mate(lv), in_send.at[lv, c], in_recv.at[my_lev, c])

    lane = lax.broadcasted_iota(jnp.int32, (SUB, LANES), 1)
    states = (state0, state_a, state_b)
    blank = jnp.zeros((PAD, SUB, LANES), jnp.float32)

    @pl.when(crew == 0)
    def _():
        for buf in states:
            for t in range(tiles):
                for h in range(halves):
                    buf[t, h, 0:PAD] = blank

    @pl.when(crew == crews - 1)
    def _():
        for buf in states:
            for t in range(tiles):
                for h in range(halves):
                    buf[t, h, PAD + deep:2 * PAD + deep] = blank

    for h in range(halves):
        for c in range(2):
            cbuf[c, h, 0:SUB, :] = jnp.zeros((SUB, LANES), jnp.float32)
            cbuf[c, h, SUB + deep:2 * SUB + deep, :] = jnp.zeros((SUB, LANES), jnp.float32)

    def wind_in(slot):
        for h in range(halves):
            landed(wrecv.at[slot * halves + h], w_recv.at[slot * halves + h])
            for c in range(2):
                base = SUB + (slot - 1) * rows
                cbuf[c, h, base:base + rows, :] = wrecv[
                    slot * halves + h, c * rows:(c + 1) * rows, :]

    for slot in range(1, span + 1):
        wind_in(slot)
    pl.when(has_down)(lambda: wind_in(0))
    pl.when(has_up)(lambda: wind_in(span + 1))
    for x0 in range(0, deep, SUB):
        for h in range(halves):
            here = cbuf[0, h, SUB + x0:SUB + x0 + SUB, :]
            left = cbuf[0, h, SUB + x0 - 1:SUB + x0 - 1 + SUB, :]
            right = cbuf[0, h, SUB + x0 + 1:SUB + x0 + 1 + SUB, :]
            for j, w in enumerate(stencil_weights(0.5 * (left + here), 0.5 * (here + right))):
                wx[j, h, x0:x0 + SUB, :] = w
        cy = [cbuf[1, h, SUB + x0:SUB + x0 + SUB, :] for h in range(halves)]
        zer = jnp.zeros((SUB, LANES), jnp.float32)
        for h in range(halves):
            nxt = pltpu.roll(cy[h + 1], LANES - 1, 1) if h + 1 < halves else zer
            prv = pltpu.roll(cy[h - 1], 1, 1) if h > 0 else zer
            up = jnp.where(lane < LANES - 1, pltpu.roll(cy[h], LANES - 1, 1), nxt)
            down = jnp.where(lane >= 1, pltpu.roll(cy[h], 1, 1), prv)
            ws = stencil_weights(0.5 * (down + cy[h]), 0.5 * (cy[h] + up))
            for j, w in enumerate(ws):
                d = j - 3
                if d > 0 and h == halves - 1:
                    w = jnp.where(lane < LANES - d, w, 0.0)
                if d < 0 and h == 0:
                    w = jnp.where(lane >= -d, w, 0.0)
                wy[j, h, x0:x0 + SUB, :] = w

    def halo(s, c, d):
        buf, own = states[s], tile_range(c)
        first, land = (deep, 0) if d == 0 else (PAD, PAD + deep)
        return remote(
            buf.at[own, :, pl.ds(first, PAD)], buf.at[own, :, pl.ds(land, PAD)],
            me + (span * halves if d == 0 else -span * halves),
            h_send.at[s, c, d], h_recv.at[s, c, d])

    def start_halo(s, c):
        pl.when(has_up)(lambda: halo(s, c, 0).start())
        pl.when(has_down)(lambda: halo(s, c, 1).start())

    def wait_halo(s, c):
        own = tile_range(c)
        pl.when(has_down)(lambda: landed(states[s].at[own, :, pl.ds(0, PAD)], h_recv.at[s, c, 0]))
        pl.when(has_up)(lambda: landed(
            states[s].at[own, :, pl.ds(PAD + deep, PAD)], h_recv.at[s, c, 1]))

    for c in range(chunks):
        for lv in range(lev):
            landed(state0.at[tile_range(c), lv % halves, pl.ds(PAD + (lv // halves) * rows, rows)],
                   in_recv.at[lv, c])
        start_halo(0, c)

    def stage(c, src, dst, off, beta, x, sums):
        wxs = [[wx[j, h, pl.ds(x, 1), :] * beta for j in range(7)] for h in range(halves)]
        wys = [[wy[j, h, pl.ds(x, 1), :] * beta for j in range(7)] for h in range(halves)]
        out = []
        for i in range(width):
            t = c * width + i
            partial, new = [], []
            for h in range(halves):
                acc = wxs[h][0] * src[t, h, x]
                for j in range(1, 7):
                    acc = acc + wxs[h][j] * src[t, h, x + j]
                mid = src[t, h, x + PAD]
                p = mid - acc
                partial.append(p)
                start = mid if src is state0 else state0[t, h, x + PAD]
                new.append(start - acc - wys[h][3] * p)
            for d in (1, 2, 3):
                up = [pltpu.roll(p, LANES - d, 1) for p in partial]
                down = [pltpu.roll(p, d, 1) for p in partial]
                for h in range(halves):
                    u = up[h] if h == halves - 1 else jnp.where(lane < LANES - d, up[h], up[h + 1])
                    w = down[h] if h == 0 else jnp.where(lane >= d, down[h], down[h - 1])
                    new[h] = new[h] - (wys[h][3 + d] * u + wys[h][3 - d] * w)
            for h in range(halves):
                dst[t, h, x + off] = new[h]
            if sums is not None:
                net, pos = sums[2 * i], sums[2 * i + 1]
                for v in new:
                    net, pos = net + v, pos + jnp.maximum(v, 0.0)
                out += [net, pos]
        return tuple(out)

    stat[...] = jnp.zeros((SUB, LANES), jnp.float32)
    for s in range(3):
        for c in range(chunks):
            wait_halo(s, c)
            if s < 2:

                @pl.loop(0, deep)
                def _(x):
                    stage(c, states[s], states[s + 1], PAD, BETAS[s], x, None)

                start_halo(s + 1, c)
                continue
            z = jnp.zeros((SUB, LANES), jnp.float32)
            sums = lax.fori_loop(
                0, deep, lambda x, v: stage(c, states[s], result, 0, BETAS[s], x, v),
                (z,) * (2 * width))
            for lv in range(lev):
                deliver(result.at[tile_range(c), lv % halves, pl.ds((lv // halves) * rows, rows)],
                        back.at[my_lev, tile_range(c)], mate(lv),
                        out_send.at[lv, c], out_recv.at[my_lev, c])
            acc = stat[...]
            for i in range(width):
                t = c * width + i
                net = jnp.sum(sums[2 * i], axis=1, keepdims=True)
                pos = jnp.sum(sums[2 * i + 1], axis=1, keepdims=True)
                acc = jnp.where(lane == t, net, jnp.where(lane == tiles + t, pos, acc))
            stat[...] = acc

    def send_stat(k, carry):
        dev = (k + me) % n
        deliver(stat, stats.at[me], dev, s_send.at[dev], s_recv.at[me])
        return carry

    lax.fori_loop(0, n, send_stat, 0)

    sub = lax.broadcasted_iota(jnp.int32, (SUB, LANES), 0)
    for t in range(tiles):
        tile = jnp.zeros((SUB, LANES), jnp.float32)
        for i in range(SUB):
            if t * SUB + i < spec:
                tile = jnp.where(sub == i, rate_ref[t * SUB + i], tile)
        prate[pl.ds(t * SUB, SUB), :] = tile
    loads[2].wait()
    loads[3].wait()
    ks = [diff_ref[lv] for lv in range(lev - 1)]
    zero = jnp.zeros((rows, LANES), jnp.float32)
    lower = [zero] + ks
    upper = ks + [zero]
    prev = None
    for lv in range(lev):
        pivot = 1.0 + lower[lv] + upper[lv]
        if lv:
            pivot = pivot + lower[lv] * prev
        inv = 1.0 / pivot
        prev = -upper[lv] * inv
        coef[0, pl.ds(lv * rows, rows), :] = inv
        coef[1, pl.ds(lv * rows, rows), :] = lower[lv]
        coef[2, pl.ds(lv * rows, rows), :] = -prev

    def stat_in(k, carry):
        landed(stats.at[k], s_recv.at[k])
        return carry

    for c in range(chunks):
        for lv in range(lev):
            landed(back.at[lv, tile_range(c)], out_recv.at[lv, c])
    lax.fori_loop(0, n, stat_in, 0)
    total = stats[0]
    for k in range(1, n):
        total = total + stats[k]

    fades = [None] * rows
    stores = []
    for t in range(tiles):
        have = min(SUB, spec - t * SUB)
        if have <= 0:
            continue
        scale = jnp.broadcast_to(
            total[:, t:t + 1] / total[:, tiles + t:tiles + t + 1], (SUB, LANES))
        rate = prate[pl.ds(t * SUB, SUB), :]
        for r in range(rows):
            emis = emis_ref[pl.ds(t * SUB * rows + r, have, stride=rows), :]
            if have < SUB:
                emis = jnp.concatenate(
                    [emis, jnp.zeros((SUB - have, LANES), jnp.float32)], axis=0)
            value = []
            for lv in range(lev):
                right = jnp.maximum(back[lv, t, r], 0.0) * scale
                if lv == 0:
                    right = right + emis
                else:
                    right = right + coef[1, pl.ds(lv * rows + r, 1), :] * value[-1]
                value.append(right * coef[0, pl.ds(lv * rows + r, 1), :])
            mixed = [None] * lev
            mixed[lev - 1] = value[lev - 1]
            for lv in range(lev - 2, -1, -1):
                mixed[lv] = value[lv] + coef[2, pl.ds(lv * rows + r, 1), :] * mixed[lv + 1]
            if t == 0:
                fade = [None] * lev
                above = jnp.zeros((1, LANES), jnp.float32)
                for lv in range(lev - 1, -1, -1):
                    mine = mixed[lv][0:1, :]
                    fade[lv] = jnp.exp((-0.5 / lev) * (above + 0.5 * mine))
                    above = above + mine
                fades[r] = fade
            for lv in range(lev):
                val = mixed[lv] * jnp.exp(-(rate * fades[r][lv]))
                out_ref[pl.ds(t * SUB * stride + lv * rows + r, have, stride=stride), :] = val[0:have]
        done = pl.ds(t * SUB * stride, have * stride)
        stores.append(pltpu.make_async_copy(out_ref.at[done], out_hbm.at[done], store_sem.at[t]))
        stores[-1].start()

    def wind_sent(o, lv, dev, at):
        pl.when(dev != me)(lambda: sent(wsend.at[lv], w_send.at[o, lv]))

    for_winds(wind_sent)
    for lv in range(lev):

        @pl.when(lv != my_lev)
        def _():
            for c in range(chunks):
                sent(send.at[lv, tile_range(c)], in_send.at[lv, c])
                sent(result.at[tile_range(c), lv % halves, pl.ds((lv // halves) * rows, rows)],
                     out_send.at[lv, c])

    for s in range(3):
        for c in range(chunks):
            own = tile_range(c)
            pl.when(has_up)(lambda: sent(states[s].at[own, :, pl.ds(deep, PAD)], h_send.at[s, c, 0]))
            pl.when(has_down)(lambda: sent(states[s].at[own, :, pl.ds(PAD, PAD)], h_send.at[s, c, 1]))

    def stat_sent(k, carry):
        sent(stat, s_send.at[(k + me) % n])
        return carry

    lax.fori_loop(1, n, stat_sent, 0)
    for store in stores:
        store.wait()


def per_device(gx_n, halves, conc, winds, diffusivity, emission, photo_rate):
    spec, lev, rows, lanes = conc.shape
    span = lev // halves
    assert span * halves == lev and gx_n % span == 0
    n = gx_n * halves
    real = -(-spec // SUB)
    chunks = CHUNKS
    width = -(-real // chunks)
    tiles = chunks * width
    deep = span * rows
    dims = (spec, lev, rows, halves, gx_n, span, tiles, chunks)
    f32 = jnp.float32
    hbm = pl.BlockSpec(memory_space=pl.ANY)
    dma = pltpu.SemaphoreType.DMA
    slots = (span + 2) * halves
    out = pl.pallas_call(
        functools.partial(kernel, dims),
        out_shape=jax.ShapeDtypeStruct((spec * lev * rows, lanes), f32),
        in_specs=[hbm] * 4 + [pl.BlockSpec(memory_space=pltpu.SMEM)],
        out_specs=hbm,
        scratch_shapes=[
            pltpu.VMEM((spec * lev * rows, lanes), f32),
            pltpu.VMEM((2 * lev * rows, lanes), f32),
            pltpu.VMEM((lev - 1, rows, lanes), f32),
            pltpu.VMEM((spec * rows, lanes), f32),
            pltpu.VMEM((lev, tiles, rows, SUB, lanes), f32),
            pltpu.VMEM((tiles, halves, deep + 2 * PAD, SUB, lanes), f32),
            pltpu.VMEM((tiles, halves, deep + 2 * PAD, SUB, lanes), f32),
            pltpu.VMEM((tiles, halves, deep + 2 * PAD, SUB, lanes), f32),
            pltpu.VMEM((tiles, halves, deep, SUB, lanes), f32),
            pltpu.VMEM((lev, tiles, rows, SUB, lanes), f32),
            pltpu.VMEM((lev, 2 * rows, lanes), f32),
            pltpu.VMEM((slots, 2 * rows, lanes), f32),
            pltpu.VMEM((2, halves, deep + 2 * SUB, lanes), f32),
            pltpu.VMEM((7, halves, deep, lanes), f32),
            pltpu.VMEM((7, halves, deep, lanes), f32),
            pltpu.VMEM((SUB, lanes), f32),
            pltpu.VMEM((n, SUB, lanes), f32),
            pltpu.VMEM((tiles * SUB, lanes), f32),
            pltpu.VMEM((3, lev * rows, lanes), f32),
            dma((4,)),
            dma((lev, chunks)), dma((lev, chunks)),
            dma((3, lev)), dma((slots,)),
            dma((3, chunks, 2)), dma((3, chunks, 2)),
            dma((lev, chunks)), dma((lev, chunks)),
            dma((n,)), dma((n,)),
            pltpu.VMEM((spec * lev * rows, lanes), f32), dma((tiles,)),
        ],
        compiler_params=pltpu.CompilerParams(collective_id=0, has_side_effects=True),
    )(
        conc.reshape(spec * lev * rows, lanes),
        winds.reshape(2 * lev * rows, lanes),
        diffusivity,
        emission.reshape(spec * rows, lanes),
        photo_rate,
    )
    return out.reshape(spec, lev, rows, lanes)


def solution(mesh):
    halves = mesh.shape["gy"]
    gx_n = mesh.shape["gx"]
    return jax.shard_map(
        functools.partial(per_device, gx_n, halves),
        mesh=mesh,
        in_specs=(
            P(None, None, ("member", "gx"), "gy"),
            P(None, None, ("member", "gx"), "gy"),
            P(None, ("member", "gx"), "gy"),
            P(None, ("member", "gx"), "gy"),
            P(),
        ),
        out_specs=P(None, None, ("member", "gx"), "gy"),
        check_vma=False,
    )
```

profile of v0, /device:TPU:0, one launch (start us, length us, event | category | flops | bytes accessed | tf_op | source)
XLA Modules:
  0.0 39.0 jit_solution(69321582885787999)
XLA Ops:
  0.0 37.1 %shard_map.55 = f32[1056,128]{1,0:T(8,128)} custom-call(f32[1056,128]{1,0:T(8,128)} %bitcast.5, f32[32,128]{1,0:T(8,128)} %bitcast.7, f32[3,4,128]{2,1,0:T(4,128)} %diff_hbm.1, f32[264,128]{1,0:T(8,128)} %bitcast.6, f32[66]{0:T(128)} %rate_ref.1), custom_call_target="tpu_custom_call" | custom-call | tf_op jit(solution)/shard_map/pallas_call | solution.py:402
  37.1 1.9 %copy.7 = f32[66,4,4,128]{3,2,1,0:T(4,128)} copy(f32[66,4,4,128]{3,2,1,0:T(4,128)} %bitcast.4) | data formatting | bytes 1081344
where the time goes:
time: 39.2 us; the launch traced here: 39 us
  Pallas kernels  37.1 us (95%)
  local copies, waits for them, and re-layouts  1.88 us (5%)
    pallas_call x1, Pallas kernels, per_device(): pl.pallas_call(functools.partial(kernel, dims), out_shape=jax.ShapeDtypeS...  37.1 us
    unnamed x1, local copies, waits for them, and re-layouts  1.88 us

commit v1 on v0

--- a/solution.py
+++ b/solution.py
@@ -351,10 +351,8 @@
                 fades[r] = fade
             for lv in range(lev):
                 val = mixed[lv] * jnp.exp(-(rate * fades[r][lv]))
-                out_ref[pl.ds(t * SUB * stride + lv * rows + r, have, stride=stride), :] = val[0:have]
+                out_hbm[pl.ds(t * SUB * stride + lv * rows + r, have, stride=stride), :] = val[0:have]
         done = pl.ds(t * SUB * stride, have * stride)
-        stores.append(pltpu.make_async_copy(out_ref.at[done], out_hbm.at[done], store_sem.at[t]))
-        stores[-1].start()
 
     def wind_sent(o, lv, dev, at):
         pl.when(dev != me)(lambda: sent(wsend.at[lv], w_send.at[o, lv]))
@@ -380,8 +378,6 @@
         return carry
 
     lax.fori_loop(1, n, stat_sent, 0)
-    for store in stores:
-        store.wait()
 
 
 def per_device(gx_n, halves, conc, winds, diffusivity, emission, photo_rate):
@@ -401,9 +397,9 @@
     slots = (span + 2) * halves
     out = pl.pallas_call(
         functools.partial(kernel, dims),
-        out_shape=jax.ShapeDtypeStruct((spec * lev * rows, lanes), f32),
+        out_shape=pltpu.VMEM((spec * lev * rows, lanes), f32),
         in_specs=[hbm] * 4 + [pl.BlockSpec(memory_space=pltpu.SMEM)],
-        out_specs=hbm,
+        out_specs=pl.BlockSpec(memory_space=pltpu.VMEM),
         scratch_shapes=[
             pltpu.VMEM((spec * lev * rows, lanes), f32),
             pltpu.VMEM((2 * lev * rows, lanes), f32),

time: 39.2 us -> 37.8 us (0.964)
  local copies, waits for them, and re-layouts: 1.88 us -> 0.8 us
  Pallas kernels: 37.1 us -> 36.7 us
    unnamed x1, local copies, waits for them, and re-layouts: 1.88 us -> 0.8 us
where the time goes in v1:
time: 37.8 us; the launch traced here: 37.5 us
  Pallas kernels  36.7 us (97%)
  local copies, waits for them, and re-layouts  0.8 us (2%)
    pallas_call x1, Pallas kernels, per_device(): pl.pallas_call(functools.partial(kernel, dims), out_shape=pltpu.VMEM((spe...  36.7 us
    unnamed x1, local copies, waits for them, and re-layouts  0.8 us

profile of v1, /device:TPU:0, one launch (start us, length us, event | category | flops | bytes accessed | tf_op | source)
XLA Modules:
  0.0 37.5 jit_solution(10827031428526845898)
XLA Ops:
  0.0 36.7 %shard_map.55 = f32[1056,128]{1,0:T(8,128)S(1)} custom-call(f32[1056,128]{1,0:T(8,128)} %bitcast.5, f32[32,128]{1,0:T(8,128)} %bitcast.7, f32[3,4,128]{2,1,0:T(4,128)} %diff_hbm.1, f32[264,128]{1,0:T(8,128)} %bitcast.6, f32[66]{0:T(128)} %rate_ref.1), custom_call_target="tpu_custom_call" | custom-call | tf_op jit(solution)/shard_map/pallas_call | solution.py:398
  36.7 0.8 %copy.7 = f32[66,4,4,128]{3,2,1,0:T(4,128)} copy(f32[66,4,4,128]{3,2,1,0:T(4,128)S(1)} %bitcast.4) | data formatting | bytes 1081344

commit v2 on v1

v2 whole, which is shorter than its diff:
```python
import functools

import jax
import jax.numpy as jnp
from jax import lax
from jax.experimental import pallas as pl
from jax.experimental.pallas import tpu as pltpu
from jax.sharding import PartitionSpec as P

BETAS = (1.0 / 3.0, 0.5, 1.0)
SUB = 8
LANES = 128
PAD = 3
WIDE = 2 * PAD
AHEAD = 11
LAG_A = 4
LAG_B = 8
LAG_U = 12
MESH = pl.DeviceIdType.MESH


def stencil_weights(km, kp):
    def face(k):
        k = k / 60.0
        a = jnp.abs(k)
        return (
            k + a,
            -8.0 * k - 5.0 * a,
            37.0 * k + 10.0 * a,
            37.0 * k - 10.0 * a,
            -8.0 * k + 5.0 * a,
            k - a,
        )

    m, p = face(km), face(kp)
    return [-m[0]] + [p[j] - m[j + 1] for j in range(5)] + [p[5]]


def kernel(dims, conc_hbm, wind_hbm, diff_hbm, emis_hbm, rate_ref, out_ref,
           diff_ref, emis_ref, state0, state1, state2, result, back,
           wrecv, cbuf, wts, part, stat, stats, scal,
           load_sem, w_send, w_recv, in_send, in_recv, d_send, r_send, a_recv,
           b_send, b_recv, out_send, out_recv, s_send, s_recv):
    spec, lev, rows, halves, gx_n, span, chunk = dims
    n = gx_n * halves
    chunks = spec // chunk
    deep = span * rows
    crews = gx_n // span
    slab, slab1, slab2 = deep + 2 * SUB, 2 * SUB, 2 * SUB
    my_gx, my_gy = lax.axis_index("gx"), lax.axis_index("gy")
    me = my_gx * halves + my_gy
    crew, seat = my_gx // span, my_gx % span
    my_lev = seat * halves + my_gy
    has_down, has_up = crew > 0, crew < crews - 1
    shift = span * halves

    def where_is(dev):
        return {"gx": dev // halves, "gy": dev % halves}

    def mate(at, half):
        return (crew * span + at) * halves + half

    barrier = pltpu.get_barrier_semaphore()

    def greet(k, carry):
        pl.semaphore_signal(barrier, inc=1, device_id=where_is((me + k) % n), device_id_type=MESH)
        return carry

    lax.fori_loop(1, n, greet, 0)
    loads = [pltpu.make_async_copy(src, dst, load_sem.at[i]) for i, (src, dst) in enumerate(
        ((diff_hbm, diff_ref), (emis_hbm, emis_ref)))]
    for load in loads:
        load.start()

    def push(src, dst, dev, s_sem, r_sem):
        pltpu.make_async_remote_copy(
            src_ref=src, dst_ref=dst, send_sem=s_sem, recv_sem=r_sem,
            device_id=where_is(dev), device_id_type=MESH).start()

    def local(src, dst, r_sem):
        pltpu.make_async_copy(src, dst, r_sem).start()

    def take(like, sem):
        pltpu.make_async_copy(like, like, sem).wait()

    def group(c):
        return pl.ds(c * chunk, chunk)

    flat0 = state0.reshape(halves * spec * slab, LANES)
    flat1 = state1.reshape(halves * chunk * slab1, LANES)
    flat2 = state2.reshape(halves * spec * slab2, LANES)
    flat_r = result.reshape(halves * spec * deep, LANES)
    flat_b = back.reshape(spec * lev * rows, LANES)
    zero = jnp.zeros((SUB, LANES), jnp.float32)
    few = jnp.zeros((SUB // 2, LANES), jnp.float32)

    def clear(first0, first2):
        @pl.loop(0, halves * spec)
        def _(i):
            flat0[pl.ds(i * slab + first0, SUB), :] = zero
            flat2[pl.ds(i * slab2 + first2, SUB // 2), :] = few

    pl.when(crew == 0)(lambda: clear(0, 0))
    pl.when(crew == crews - 1)(lambda: clear(SUB + deep, SUB // 2 + deep))
    for h in range(halves):
        for c in range(2):
            cbuf[c, h, 0:SUB, :] = zero
            cbuf[c, h, SUB + deep:2 * SUB + deep, :] = zero
    part[...] = jnp.zeros_like(part)
    stat[...] = zero

    pl.semaphore_wait(barrier, n - 1)

    own_rows = pl.ds(SUB + seat * rows, rows)

    def send_in(c):
        dst = state0.at[my_gy, group(c), own_rows]
        for k in range(1, span):
            at = (seat + k) % span
            for h in range(halves):
                push(conc_hbm.at[group(c), at * halves + h], dst, mate(at, h),
                     in_send.at[k * halves + h], in_recv.at[seat, c])
        for k in range(1, halves):
            h = (my_gy + k) % halves
            push(conc_hbm.at[group(c), seat * halves + h], dst, mate(seat, h),
                 in_send.at[k], in_recv.at[seat, c])
        local(conc_hbm.at[group(c), my_lev], dst, in_recv.at[seat, c])

    def reach(at, up):
        if up:
            first = max(0, deep - WIDE - at * rows)
            return first, rows - first, SUB - deep + at * rows + first
        return 0, max(0, min(rows, WIDE - at * rows)), SUB + deep + at * rows

    def each_way(act):
        for up, cond in ((1, has_up), (0, has_down)):
            for at in range(span):
                pl.when(cond & (seat == at))(functools.partial(act, up, at))

    def send_direct(c):
        def act(up, at):
            first, count, land = reach(at, up)
            if count > 0:
                for h in range(halves):
                    push(conc_hbm.at[group(c), at * halves + h, pl.ds(first, count)],
                         state0.at[my_gy, group(c), pl.ds(land, count)],
                         mate(at, h) + (shift if up else -shift),
                         d_send.at[up, h], a_recv.at[up, c])

        each_way(act)

    def send_relay(c):
        def act(up, at):
            for other in range(span):
                first, count, land = reach(other, up)
                if other != at and count > 0:
                    push(state0.at[:, group(c), pl.ds(SUB + other * rows + first, count)],
                         state0.at[:, group(c), pl.ds(land, count)],
                         me + (shift if up else -shift), r_send.at[up], a_recv.at[up, c])

        each_way(act)

    sides = ((0, None, None), (1, has_up & (seat == span - 1), 0),
             (-1, has_down & (seat == 0), span + 1))

    def for_winds(act):
        for o, (step, cond, slot) in enumerate(sides):
            at = seat + 1 if slot is None else slot
            for lv in range(lev):
                dev = mate(lv // halves, lv % halves) + step * shift
                if cond is None:
                    pl.when(dev != me)(functools.partial(act, o, lv, dev, at))
                else:
                    pl.when(cond)(functools.partial(act, o, lv, dev, at))

    for_winds(lambda o, lv, dev, at: push(
        wind_hbm.at[:, lv], wrecv.at[at * halves + my_gy], dev, w_send.at[o, lv],
        w_recv.at[at * halves + my_gy]))
    local(wind_hbm.at[:, my_lev], wrecv.at[(seat + 1) * halves + my_gy],
          w_recv.at[(seat + 1) * halves + my_gy])

    @pl.loop(0, chunks)
    def _(c):
        send_in(c)
        pl.when(c < AHEAD)(lambda: send_direct(c))

    lane = lax.broadcasted_iota(jnp.int32, (SUB, LANES), 1)
    sub = lax.broadcasted_iota(jnp.int32, (SUB, LANES), 0)

    for load in loads:
        load.wait()
    ks = [diff_ref[lv] for lv in range(lev - 1)]
    none = jnp.zeros((rows, LANES), jnp.float32)
    lower, upper = [none] + ks, ks + [none]
    inv, ratio = [], []
    for lv in range(lev):
        pivot = 1.0 + lower[lv] + upper[lv]
        if lv:
            pivot = pivot - lower[lv] * ratio[-1]
        inv.append(1.0 / pivot)
        ratio.append(upper[lv] * inv[lv])
    inverse = [[None] * lev for _ in range(lev)]
    for j in range(lev):
        val = [none] * lev
        for lv in range(j, lev):
            val[lv] = inv[lv] if lv == j else lower[lv] * val[lv - 1] * inv[lv]
        for lv in range(lev - 1, -1, -1):
            inverse[lv][j] = val[lv] if lv == lev - 1 else val[lv] + ratio[lv] * inverse[lv + 1][j]
    pairs = lev // 2

    def duo(a, b):
        return jnp.concatenate([a, b], axis=0)

    mats = [[(duo(inverse[2 * o][2 * i], inverse[2 * o + 1][2 * i + 1]),
              duo(inverse[2 * o][2 * i + 1], inverse[2 * o + 1][2 * i]))
             for i in range(pairs)] for o in range(pairs)]
    first_col = [duo(inverse[2 * o][0], inverse[2 * o + 1][0]) for o in range(pairs)]

    def flip(v):
        return pltpu.roll(v, SUB // 2, 0)

    low = sub < SUB // 2

    @pl.loop(0, spec // 2)
    def _(s):
        e = emis_ref[pl.ds(s * SUB, SUB), :]
        f = flip(e)
        for k, v in enumerate((jnp.where(low, e, f), jnp.where(low, f, e))):
            for o in range(pairs):
                out_ref[pl.ds((2 * s + k) * lev * rows + o * SUB, SUB), :] = first_col[o] * v

    def wind_in(slot):
        for h in range(halves):
            take(wrecv.at[slot * halves + h], w_recv.at[slot * halves + h])
            for c in range(2):
                base = SUB + (slot - 1) * rows
                cbuf[c, h, base:base + rows, :] = wrecv[slot * halves + h, c]

    for slot in range(1, span + 1):
        wind_in(slot)
    pl.when(has_down)(lambda: wind_in(0))
    pl.when(has_up)(lambda: wind_in(span + 1))

    passes = ((0, -PAD), (0, deep - SUB + PAD), (1, 0), (2, 0))
    for q, (s, r0) in enumerate(passes):
        at_row = crew * deep + r0 + sub
        inside = (at_row >= 0) & (at_row < crews * deep)
        for h in range(halves):
            here, left, right = (cbuf[0, h, SUB + r0 + d:2 * SUB + r0 + d, :] for d in (0, -1, 1))
            for j, w in enumerate(stencil_weights(0.5 * (left + here), 0.5 * (here + right))):
                wts[q, h, j] = jnp.where(inside, w, 0.0) * BETAS[s]
        cy = [cbuf[1, h, SUB + r0:2 * SUB + r0, :] for h in range(halves)]
        for h in range(halves):
            nxt = pltpu.roll(cy[h + 1], LANES - 1, 1) if h + 1 < halves else zero
            prv = pltpu.roll(cy[h - 1], 1, 1) if h > 0 else zero
            up = jnp.where(lane < LANES - 1, pltpu.roll(cy[h], LANES - 1, 1), nxt)
            down = jnp.where(lane >= 1, pltpu.roll(cy[h], 1, 1), prv)
            ws = stencil_weights(0.5 * (down + cy[h]), 0.5 * (cy[h] + up))
            for j, w in enumerate(ws):
                d = j - 3
                if d > 0 and h == halves - 1:
                    w = jnp.where(lane < LANES - d, w, 0.0)
                if d < 0 and h == 0:
                    w = jnp.where(lane >= -d, w, 0.0)
                wts[q, h, 7 + j] = w * BETAS[s]

    def step(q, count, src, src_at, start, start_at, put):
        wx = [[wts[q, h, j] for j in range(7)] for h in range(halves)]
        wy = [[wts[q, h, 7 + j] for j in range(7)] for h in range(halves)]
        for i in range(count):
            partial, new = [], []
            for h in range(halves):
                base = src_at(h, i)
                mid = None
                acc = None
                for j in range(7):
                    v = src[pl.ds(base + j, SUB), :]
                    if j == PAD:
                        mid = v
                    acc = wx[h][j] * v if acc is None else acc + wx[h][j] * v
                p = mid - acc
                partial.append(p)
                begin = mid if start is None else start[pl.ds(start_at(h, i), SUB), :]
                new.append(begin - acc - wy[h][3] * p)
            for d in (1, 2, 3):
                up = [pltpu.roll(p, LANES - d, 1) for p in partial]
                down = [pltpu.roll(p, d, 1) for p in partial]
                for h in range(halves):
                    u = up[h] if h == halves - 1 else jnp.where(lane < LANES - d, up[h], up[h + 1])
                    w = down[h] if h == 0 else jnp.where(lane >= d, down[h], down[h - 1])
                    new[h] = new[h] - (wy[h][3 + d] * u + wy[h][3 - d] * w)
            put(i, new)

    def at0(c):
        return lambda h, i: (h * spec + c * chunk + i) * slab

    def send_edge(c):
        for up, cond in ((1, has_up), (0, has_down)):
            first = SUB // 2 + (deep - PAD if up else 0)
            land = SUB // 2 + (-PAD if up else deep)
            pl.when(cond)(functools.partial(
                push, state2.at[:, group(c), pl.ds(first, PAD)],
                state2.at[:, group(c), pl.ds(land, PAD)],
                me + (shift if up else -shift), b_send.at[up], b_recv.at[up, c]))

    def early(c):
        take(state0.at[:, group(c), pl.ds(0, rows)], in_recv.at[seat, c])
        pl.when(has_down)(lambda: take(state0.at[:, group(c), pl.ds(0, WIDE)], a_recv.at[1, c]))
        pl.when(has_up)(lambda: take(state0.at[:, group(c), pl.ds(0, WIDE)], a_recv.at[0, c]))
        base = at0(c)
        for q in (0, 1):
            off = passes[q][1]

            def put(i, new, off=off):
                for h in range(halves):
                    flat1[pl.ds((h * chunk + i) * slab1 + off + PAD, SUB), :] = new[h]

            step(q, chunk, flat0, lambda h, i: base(h, i) + SUB + off - PAD, None, None, put)

        def put(i, new):
            for h in range(halves):
                flat2[pl.ds((h * spec + c * chunk + i) * slab2 + SUB // 2, SUB), :] = new[h]

        step(2, chunk, flat1, lambda h, i: (h * chunk + i) * slab1, flat0,
             lambda h, i: base(h, i) + SUB, put)
        send_edge(c)

    def late(c):
        pl.when(has_down)(lambda: take(state2.at[:, group(c), pl.ds(0, PAD)], b_recv.at[1, c]))
        pl.when(has_up)(lambda: take(state2.at[:, group(c), pl.ds(0, PAD)], b_recv.at[0, c]))
        base = at0(c)

        def put(i, new):
            net, pos = None, None
            for h in range(halves):
                flat_r[pl.ds((h * spec + c * chunk + i) * deep, SUB), :] = new[h]
                p = jnp.maximum(new[h], 0.0)
                net, pos = (new[h], p) if net is None else (net + new[h], pos + p)
            part[0, pl.ds(i * SUB, SUB), :] = net
            part[1, pl.ds(i * SUB, SUB), :] = pos

        step(3, chunk, flat2, lambda h, i: (h * spec + c * chunk + i) * slab2 + SUB // 2 - PAD,
             flat0, lambda h, i: base(h, i) + SUB, put)
        for k in range(1, span * halves):
            m = (my_lev + k) % (span * halves)
            push(result.at[m % halves, group(c), pl.ds((m // halves) * rows, rows)],
                 back.at[group(c), my_lev], mate(m // halves, m % halves),
                 out_send.at[k], out_recv.at[c])
        local(result.at[my_gy, group(c), pl.ds(seat * rows, rows)],
              back.at[group(c), my_lev], out_recv.at[c])
        acc = stat[...]
        for o in range(2):
            tot = part[o, pl.ds(0, SUB, stride=SUB), :]
            for r in range(1, SUB):
                tot = tot + part[o, pl.ds(r, SUB, stride=SUB), :]
            acc = jnp.where(lane == c + o * (LANES // 2), jnp.sum(tot, axis=1, keepdims=True), acc)
        stat[...] = acc

    def solve(c):
        take(back.at[group(c)], out_recv.at[c])
        for i in range(chunk):
            base = (c * chunk + i) * lev * rows
            tiles = [jnp.maximum(flat_b[pl.ds(base + o * SUB, SUB), :], 0.0) for o in range(pairs)]
            swaps = [flip(t) for t in tiles]
            for o in range(pairs):
                acc = None
                for k in range(pairs):
                    term = mats[o][k][0] * tiles[k] + mats[o][k][1] * swaps[k]
                    acc = term if acc is None else acc + term
                flat_b[pl.ds(base + o * SUB, SUB), :] = acc

    @pl.loop(0, chunks + LAG_U)
    def _(i):
        @pl.when(i < chunks)
        def _():
            for k in range(1, span):
                at = (seat + k) % span
                take(state0.at[:, group(i), pl.ds(0, rows)], in_recv.at[at, i])
            send_relay(i)
            pl.when(i + AHEAD < chunks)(lambda: send_direct(i + AHEAD))

        @pl.when((i >= LAG_A) & (i < LAG_A + chunks))
        def _():
            early(i - LAG_A)

        @pl.when((i >= LAG_B) & (i < LAG_B + chunks))
        def _():
            late(i - LAG_B)

        @pl.when(i == LAG_B + chunks - 1)
        def _():
            def send_stat(k, carry):
                dev = (k + me) % n
                push(stat, stats.at[me], dev, s_send, s_recv)
                return carry

            lax.fori_loop(1, n, send_stat, 0)
            stats[pl.ds(me, 1)] = stat[...][None]

        @pl.when(i >= LAG_U)
        def _():
            solve(i - LAG_U)

    for_winds(lambda o, lv, dev, at: take(wrecv.at[0], w_send.at[o, lv]))
    whole = state0.at[0, :, pl.ds(0, rows)]
    for k in range(1, span * halves):
        take(whole, in_send.at[k])
        take(whole, out_send.at[k])

    def drain(up, at):
        _, count, _ = reach(at, up)
        if count > 0:
            for h in range(halves):
                take(state0.at[0, :, pl.ds(0, count)], d_send.at[up, h])
        total = sum(reach(other, up)[1] for other in range(span) if other != at)
        if total > 0:
            take(state0.at[:, :, pl.ds(0, total)], r_send.at[up])

    each_way(drain)
    for up, cond in ((1, has_up), (0, has_down)):
        pl.when(cond)(functools.partial(take, state2.at[:, :, pl.ds(0, PAD)], b_send.at[up]))

    others = stats.at[pl.ds(0, n - 1)]
    take(others, s_send)
    take(others, s_recv)
    total = stats[0]
    for k in range(1, n):
        total = total + stats[k]
    quotient = total / pltpu.roll(total, LANES // 2, 1)
    for c in range(chunks):
        scal[pl.ds(c * SUB, SUB), :] = jnp.broadcast_to(quotient[:, c:c + 1], (SUB, LANES))

    def mixed(s, scale, o):
        at = pl.ds(s * lev * rows + o * SUB, SUB)
        return scale * flat_b[at, :] + out_ref[at, :]

    m0 = [mixed(0, scal[0:1, :], o) for o in range(pairs)]
    above = zero
    fades = [None] * pairs
    for o in range(pairs - 1, -1, -1):
        turn = flip(m0[o])
        col = above + 0.5 * m0[o] + jnp.where(low, turn, 0.0)
        fades[o] = jnp.exp((-0.5 / lev) * col)
        above = above + (m0[o] + turn)

    @pl.loop(0, chunks)
    def _(c):
        for i in range(chunk):
            s = c * chunk + i
            scale = scal[pl.ds(c * SUB + i, 1), :]
            rate = rate_ref[s]
            for o in range(pairs):
                out_ref[pl.ds(s * lev * rows + o * SUB, SUB), :] = (
                    mixed(s, scale, o) * jnp.exp(-(rate * fades[o])))


def per_device(gx_n, halves, conc, winds, diffusivity, emission, photo_rate):
    spec, lev, rows, lanes = conc.shape
    span = lev // halves
    assert span * halves == lev and gx_n % span == 0 and lev % 2 == 0
    assert lanes == LANES and 2 * rows == SUB and span * rows == SUB and spec % 2 == 0
    n = gx_n * halves
    chunk = max(d for d in range(1, SUB + 1) if spec % d == 0)
    chunks = spec // chunk
    assert chunks <= LANES // 2
    deep = span * rows
    dims = (spec, lev, rows, halves, gx_n, span, chunk)
    f32 = jnp.float32
    hbm = pl.BlockSpec(memory_space=pl.ANY)
    dma = pltpu.SemaphoreType.DMA
    slots = (span + 2) * halves
    out = pl.pallas_call(
        functools.partial(kernel, dims),
        out_shape=pltpu.VMEM((spec * lev * rows, lanes), f32),
        in_specs=[hbm] * 4 + [pl.BlockSpec(memory_space=pltpu.SMEM)],
        out_specs=pl.BlockSpec(memory_space=pltpu.VMEM),
        scratch_shapes=[
            pltpu.VMEM((lev - 1, rows, lanes), f32),
            pltpu.VMEM((spec * rows, lanes), f32),
            pltpu.VMEM((halves, spec, deep + 2 * SUB, lanes), f32),
            pltpu.VMEM((halves, chunk, 2 * SUB, lanes), f32),
            pltpu.VMEM((halves, spec, 2 * SUB, lanes), f32),
            pltpu.VMEM((halves, spec, deep, lanes), f32),
            pltpu.VMEM((spec, lev, rows, lanes), f32),
            pltpu.VMEM((slots, 2, rows, lanes), f32),
            pltpu.VMEM((2, halves, deep + 2 * SUB, lanes), f32),
            pltpu.VMEM((4, halves, 14, SUB, lanes), f32),
            pltpu.VMEM((2, SUB * SUB, lanes), f32),
            pltpu.VMEM((SUB, lanes), f32),
            pltpu.VMEM((n, SUB, lanes), f32),
            pltpu.VMEM((chunks * SUB, lanes), f32),
            dma((2,)),
            dma((3, lev)), dma((slots,)),
            dma((lev,)), dma((span, chunks)),
            dma((2, halves)), dma((2,)), dma((2, chunks)),
            dma((2,)), dma((2, chunks)),
            dma((lev,)), dma((chunks,)),
            dma(()), dma(()),
        ],
        compiler_params=pltpu.CompilerParams(collective_id=0, has_side_effects=True),
    )(
        conc,
        winds,
        diffusivity,
        emission.reshape(spec * rows, lanes),
        photo_rate,
    )
    return out.reshape(spec, lev, rows, lanes)


def solution(mesh):
    halves = mesh.shape["gy"]
    gx_n = mesh.shape["gx"]
    return jax.shard_map(
        functools.partial(per_device, gx_n, halves),
        mesh=mesh,
        in_specs=(
            P(None, None, ("member", "gx"), "gy"),
            P(None, None, ("member", "gx"), "gy"),
            P(None, ("member", "gx"), "gy"),
            P(None, ("member", "gx"), "gy"),
            P(),
        ),
        out_specs=P(None, None, ("member", "gx"), "gy"),
        check_vma=False,
    )
```

time: 37.8 us -> 32.9 us (0.87)
  Pallas kernels: 36.7 us -> 32 us
    pallas_call x1, Pallas kernels: 36.7 us -> 32 us  [per_device(): pl.pallas_call(functools.partial(kernel, dims), out_shape=pltpu.VMEM((spe...]
where the time goes in v2:
time: 32.9 us; the launch traced here: 32.8 us
  Pallas kernels  32 us (97%)
  local copies, waits for them, and re-layouts  0.8 us (2%)
    pallas_call x1, Pallas kernels, per_device(): pl.pallas_call(functools.partial(kernel, dims), out_shape=pltpu.VMEM((spe...  32 us
    unnamed x1, local copies, waits for them, and re-layouts  0.8 us

profile of v2, /device:TPU:0, one launch (start us, length us, event | category | flops | bytes accessed | tf_op | source)
XLA Modules:
  0.0 32.8 jit_solution(11415780210201419976)
XLA Ops:
  0.0 32.0 %shard_map.55 = f32[1056,128]{1,0:T(8,128)S(1)} custom-call(f32[66,4,4,128]{3,2,1,0:T(4,128)} %conc_hbm.1, f32[2,4,4,128]{3,2,1,0:T(4,128)} %wind_hbm.1, f32[3,4,128]{2,1,0:T(4,128)} %diff_hbm.1, f32[264,128]{1,0:T(8,128)} %bitcast.3, f32[66]{0:T(128)} %rate_ref.1), custom_call_target="tpu_custom_call" | custom-call | tf_op jit(solution)/shard_map/pallas_call | solution.py:472
  32.0 0.8 %copy.7 = f32[66,4,4,128]{3,2,1,0:T(4,128)} copy(f32[66,4,4,128]{3,2,1,0:T(4,128)S(1)} %bitcast.2) | data formatting | bytes 1081344

commit v3 on v2

--- a/solution.py
+++ b/solution.py
@@ -12,10 +12,11 @@
 LANES = 128
 PAD = 3
 WIDE = 2 * PAD
-AHEAD = 11
-LAG_A = 4
-LAG_B = 8
-LAG_U = 12
+AHEAD = 6
+LAG_A = 5
+LAG_B = 10
+LAG_U = 15
+WIDTH = 11
 MESH = pl.DeviceIdType.MESH
 
 
@@ -36,14 +37,15 @@
     return [-m[0]] + [p[j] - m[j + 1] for j in range(5)] + [p[5]]
 
 
-def kernel(dims, conc_hbm, wind_hbm, diff_hbm, emis_hbm, rate_ref, out_ref,
-           diff_ref, emis_ref, state0, state1, state2, result, back,
+def kernel(dims, conc_hbm, wind_hbm, diff_hbm, emis_hbm, rate_hbm, out_ref,
+           rate_ref, diff_ref, emis_ref, state0, state1, state2, result, back,
            wrecv, cbuf, wts, part, stat, stats, scal,
            load_sem, w_send, w_recv, in_send, in_recv, d_send, r_send, a_recv,
            b_send, b_recv, out_send, out_recv, s_send, s_recv):
     spec, lev, rows, halves, gx_n, span, chunk = dims
     n = gx_n * halves
     chunks = spec // chunk
+    groups = -(-chunk // SUB)
     deep = span * rows
     crews = gx_n // span
     slab, slab1, slab2 = deep + 2 * SUB, 2 * SUB, 2 * SUB
@@ -63,12 +65,12 @@
     barrier = pltpu.get_barrier_semaphore()
 
     def greet(k, carry):
-        pl.semaphore_signal(barrier, inc=1, device_id=where_is((me + k) % n), device_id_type=MESH)
+        pl.semaphore_signal(barrier, inc=1, device_id=where_is((me + n - k) % n), device_id_type=MESH)
         return carry
 
     lax.fori_loop(1, n, greet, 0)
     loads = [pltpu.make_async_copy(src, dst, load_sem.at[i]) for i, (src, dst) in enumerate(
-        ((diff_hbm, diff_ref), (emis_hbm, emis_ref)))]
+        ((diff_hbm, diff_ref), (emis_hbm, emis_ref), (rate_hbm, rate_ref)))]
     for load in loads:
         load.start()
 
@@ -93,21 +95,6 @@
     flat_b = back.reshape(spec * lev * rows, LANES)
     zero = jnp.zeros((SUB, LANES), jnp.float32)
     few = jnp.zeros((SUB // 2, LANES), jnp.float32)
-
-    def clear(first0, first2):
-        @pl.loop(0, halves * spec)
-        def _(i):
-            flat0[pl.ds(i * slab + first0, SUB), :] = zero
-            flat2[pl.ds(i * slab2 + first2, SUB // 2), :] = few
-
-    pl.when(crew == 0)(lambda: clear(0, 0))
-    pl.when(crew == crews - 1)(lambda: clear(SUB + deep, SUB // 2 + deep))
-    for h in range(halves):
-        for c in range(2):
-            cbuf[c, h, 0:SUB, :] = zero
-            cbuf[c, h, SUB + deep:2 * SUB + deep, :] = zero
-    part[...] = jnp.zeros_like(part)
-    stat[...] = zero
 
     pl.semaphore_wait(barrier, n - 1)
 
@@ -181,8 +168,24 @@
 
     @pl.loop(0, chunks)
     def _(c):
+        pl.when(c < AHEAD)(lambda: send_direct(c))
         send_in(c)
-        pl.when(c < AHEAD)(lambda: send_direct(c))
+
+    def clear(first0, first2):
+        @pl.loop(0, halves * chunks)
+        def _(i):
+            for k in range(chunk):
+                flat0[pl.ds((i * chunk + k) * slab + first0, SUB), :] = zero
+                flat2[pl.ds((i * chunk + k) * slab2 + first2, SUB // 2), :] = few
+
+    pl.when(crew == 0)(lambda: clear(0, 0))
+    pl.when(crew == crews - 1)(lambda: clear(SUB + deep, SUB // 2 + deep))
+    for h in range(halves):
+        for c in range(2):
+            cbuf[c, h, 0:SUB, :] = zero
+            cbuf[c, h, SUB + deep:2 * SUB + deep, :] = zero
+    part[...] = jnp.zeros_like(part)
+    stat[...] = zero
 
     lane = lax.broadcasted_iota(jnp.int32, (SUB, LANES), 1)
     sub = lax.broadcasted_iota(jnp.int32, (SUB, LANES), 0)
@@ -341,6 +344,27 @@
 
         step(3, chunk, flat2, lambda h, i: (h * spec + c * chunk + i) * slab2 + SUB // 2 - PAD,
              flat0, lambda h, i: base(h, i) + SUB, put)
+        acc = stat[...]
+        for o in range(2):
+            for g in range(groups):
+                first = g * SUB * SUB
+                tot = part[o, pl.ds(first, SUB, stride=SUB), :]
+                for r in range(1, SUB):
+                    tot = tot + part[o, pl.ds(first + r, SUB, stride=SUB), :]
+                acc = jnp.where(lane == c * groups + g + o * (LANES // 2),
+                                jnp.sum(tot, axis=1, keepdims=True), acc)
+        stat[...] = acc
+
+        @pl.when(c == chunks - 1)
+        def _():
+            def send_stat(k, carry):
+                dev = (k + me) % n
+                push(stat, stats.at[me], dev, s_send, s_recv)
+                return carry
+
+            lax.fori_loop(1, n, send_stat, 0)
+            stats[pl.ds(me, 1)] = stat[...][None]
+
         for k in range(1, span * halves):
             m = (my_lev + k) % (span * halves)
             push(result.at[m % halves, group(c), pl.ds((m // halves) * rows, rows)],
@@ -348,13 +372,6 @@
                  out_send.at[k], out_recv.at[c])
         local(result.at[my_gy, group(c), pl.ds(seat * rows, rows)],
               back.at[group(c), my_lev], out_recv.at[c])
-        acc = stat[...]
-        for o in range(2):
-            tot = part[o, pl.ds(0, SUB, stride=SUB), :]
-            for r in range(1, SUB):
-                tot = tot + part[o, pl.ds(r, SUB, stride=SUB), :]
-            acc = jnp.where(lane == c + o * (LANES // 2), jnp.sum(tot, axis=1, keepdims=True), acc)
-        stat[...] = acc
 
     def solve(c):
         take(back.at[group(c)], out_recv.at[c])
@@ -387,16 +404,6 @@
         def _():
             late(i - LAG_B)
 
-        @pl.when(i == LAG_B + chunks - 1)
-        def _():
-            def send_stat(k, carry):
-                dev = (k + me) % n
-                push(stat, stats.at[me], dev, s_send, s_recv)
-                return carry
-
-            lax.fori_loop(1, n, send_stat, 0)
-            stats[pl.ds(me, 1)] = stat[...][None]
-
         @pl.when(i >= LAG_U)
         def _():
             solve(i - LAG_U)
@@ -427,7 +434,7 @@
     for k in range(1, n):
         total = total + stats[k]
     quotient = total / pltpu.roll(total, LANES // 2, 1)
-    for c in range(chunks):
+    for c in range(chunks * groups):
         scal[pl.ds(c * SUB, SUB), :] = jnp.broadcast_to(quotient[:, c:c + 1], (SUB, LANES))
 
     def mixed(s, scale, o):
@@ -447,7 +454,7 @@
     def _(c):
         for i in range(chunk):
             s = c * chunk + i
-            scale = scal[pl.ds(c * SUB + i, 1), :]
+            scale = scal[pl.ds(c * groups * SUB + i, 1), :]
             rate = rate_ref[s]
             for o in range(pairs):
                 out_ref[pl.ds(s * lev * rows + o * SUB, SUB), :] = (
@@ -460,9 +467,10 @@
     assert span * halves == lev and gx_n % span == 0 and lev % 2 == 0
     assert lanes == LANES and 2 * rows == SUB and span * rows == SUB and spec % 2 == 0
     n = gx_n * halves
-    chunk = max(d for d in range(1, SUB + 1) if spec % d == 0)
+    chunk = max(d for d in range(1, WIDTH + 1) if spec % d == 0)
     chunks = spec // chunk
-    assert chunks <= LANES // 2
+    groups = -(-chunk // SUB)
+    assert chunks * groups <= LANES // 2
     deep = span * rows
     dims = (spec, lev, rows, halves, gx_n, span, chunk)
     f32 = jnp.float32
@@ -472,9 +480,10 @@
     out = pl.pallas_call(
         functools.partial(kernel, dims),
         out_shape=pltpu.VMEM((spec * lev * rows, lanes), f32),
-        in_specs=[hbm] * 4 + [pl.BlockSpec(memory_space=pltpu.SMEM)],
+        in_specs=[hbm] * 5,
         out_specs=pl.BlockSpec(memory_space=pltpu.VMEM),
         scratch_shapes=[
+            pltpu.SMEM((spec,), f32),
             pltpu.VMEM((lev - 1, rows, lanes), f32),
             pltpu.VMEM((spec * rows, lanes), f32),
             pltpu.VMEM((halves, spec, deep + 2 * SUB, lanes), f32),
@@ -485,11 +494,11 @@
             pltpu.VMEM((slots, 2, rows, lanes), f32),
             pltpu.VMEM((2, halves, deep + 2 * SUB, lanes), f32),
             pltpu.VMEM((4, halves, 14, SUB, lanes), f32),
-            pltpu.VMEM((2, SUB * SUB, lanes), f32),
+            pltpu.VMEM((2, groups * SUB * SUB, lanes), f32),
             pltpu.VMEM((SUB, lanes), f32),
             pltpu.VMEM((n, SUB, lanes), f32),
-            pltpu.VMEM((chunks * SUB, lanes), f32),
-            dma((2,)),
+            pltpu.VMEM((chunks * groups * SUB, lanes), f32),
+            dma((3,)),
             dma((3, lev)), dma((slots,)),
             dma((lev,)), dma((span, chunks)),
             dma((2, halves)), dma((2,)), dma((2, chunks)),

time: 32.9 us -> 28.6 us (0.87)
  Pallas kernels: 32 us -> 27.6 us
    pallas_call x1, Pallas kernels: 32 us -> 27.6 us  [per_device(): pl.pallas_call(functools.partial(kernel, dims), out_shape=pltpu.VMEM((spe...]
where the time goes in v3:
time: 28.6 us; the launch traced here: 28.5 us
  Pallas kernels  27.6 us (97%)
  local copies, waits for them, and re-layouts  0.8 us (3%)
    pallas_call x1, Pallas kernels, per_device(): pl.pallas_call(functools.partial(kernel, dims), out_shape=pltpu.VMEM((spe...  27.6 us
    unnamed x1, local copies, waits for them, and re-layouts  0.8 us

profile of v3, /device:TPU:0, one launch (start us, length us, event | category | flops | bytes accessed | tf_op | source)
XLA Modules:
  0.0 28.5 jit_solution(6476826321876853289)
XLA Ops:
  0.0 27.6 %shard_map.55 = f32[1056,128]{1,0:T(8,128)S(1)} custom-call(f32[66,4,4,128]{3,2,1,0:T(4,128)} %conc_hbm.1, f32[2,4,4,128]{3,2,1,0:T(4,128)} %wind_hbm.1, f32[3,4,128]{2,1,0:T(4,128)} %diff_hbm.1, f32[264,128]{1,0:T(8,128)} %bitcast.3, f32[66]{0:T(128)} %rate_hbm.1), custom_call_target="tpu_custom_call" | custom-call | tf_op jit(solution)/shard_map/pallas_call | solution.py:480
  27.7 0.8 %copy.7 = f32[66,4,4,128]{3,2,1,0:T(4,128)} copy(f32[66,4,4,128]{3,2,1,0:T(4,128)S(1)} %bitcast.2) | data formatting | bytes 1081344

commit v4 on v3

--- a/solution.py
+++ b/solution.py
@@ -12,7 +12,6 @@
 LANES = 128
 PAD = 3
 WIDE = 2 * PAD
-AHEAD = 6
 LAG_A = 5
 LAG_B = 10
 LAG_U = 15
@@ -40,8 +39,8 @@
 def kernel(dims, conc_hbm, wind_hbm, diff_hbm, emis_hbm, rate_hbm, out_ref,
            rate_ref, diff_ref, emis_ref, state0, state1, state2, result, back,
            wrecv, cbuf, wts, part, stat, stats, scal,
-           load_sem, w_send, w_recv, in_send, in_recv, d_send, r_send, a_recv,
-           b_send, b_recv, out_send, out_recv, s_send, s_recv):
+           load_sem, w_send, w_recv, in_send, in_recv, own_recv, d_send, d_recv, r_send, a_recv,
+           b_send, b_recv, out_send, out_recv, s_send, s_recv, token):
     spec, lev, rows, halves, gx_n, span, chunk = dims
     n = gx_n * halves
     chunks = spec // chunk
@@ -64,11 +63,18 @@
 
     barrier = pltpu.get_barrier_semaphore()
 
-    def greet(k, carry):
-        pl.semaphore_signal(barrier, inc=1, device_id=where_is((me + n - k) % n), device_id_type=MESH)
-        return carry
-
-    lax.fori_loop(1, n, greet, 0)
+    def greet(dev):
+        pl.semaphore_signal(barrier, inc=1, device_id=where_is(dev), device_id_type=MESH)
+
+    for k in range(1, lev):
+        m = (my_lev + k) % lev
+        greet(mate(m // halves, m % halves))
+    for cond, move in ((has_down, -shift), (has_up, shift)):
+        @pl.when(cond)
+        def _():
+            for m in range(lev):
+                greet(mate(m // halves, m % halves) + move)
+
     loads = [pltpu.make_async_copy(src, dst, load_sem.at[i]) for i, (src, dst) in enumerate(
         ((diff_hbm, diff_ref), (emis_hbm, emis_ref), (rate_hbm, rate_ref)))]
     for load in loads:
@@ -96,7 +102,7 @@
     zero = jnp.zeros((SUB, LANES), jnp.float32)
     few = jnp.zeros((SUB // 2, LANES), jnp.float32)
 
-    pl.semaphore_wait(barrier, n - 1)
+    pl.semaphore_wait(barrier, lev - 1 + jnp.where(has_down, lev, 0) + jnp.where(has_up, lev, 0))
 
     own_rows = pl.ds(SUB + seat * rows, rows)
 
@@ -107,11 +113,13 @@
             for h in range(halves):
                 push(conc_hbm.at[group(c), at * halves + h], dst, mate(at, h),
                      in_send.at[k * halves + h], in_recv.at[seat, c])
+
+    def send_own():
+        dst = state0.at[my_gy, :, own_rows]
         for k in range(1, halves):
             h = (my_gy + k) % halves
-            push(conc_hbm.at[group(c), seat * halves + h], dst, mate(seat, h),
-                 in_send.at[k], in_recv.at[seat, c])
-        local(conc_hbm.at[group(c), my_lev], dst, in_recv.at[seat, c])
+            push(conc_hbm.at[:, seat * halves + h], dst, mate(seat, h), in_send.at[k], own_recv)
+        local(conc_hbm.at[:, my_lev], dst, own_recv)
 
     def reach(at, up):
         if up:
@@ -119,20 +127,20 @@
             return first, rows - first, SUB - deep + at * rows + first
         return 0, max(0, min(rows, WIDE - at * rows)), SUB + deep + at * rows
 
-    def each_way(act):
-        for up, cond in ((1, has_up), (0, has_down)):
+    def each_way(act, landing=False):
+        for up, cond in ((1, has_down if landing else has_up), (0, has_up if landing else has_down)):
             for at in range(span):
                 pl.when(cond & (seat == at))(functools.partial(act, up, at))
 
-    def send_direct(c):
+    def send_direct():
         def act(up, at):
             first, count, land = reach(at, up)
             if count > 0:
                 for h in range(halves):
-                    push(conc_hbm.at[group(c), at * halves + h, pl.ds(first, count)],
-                         state0.at[my_gy, group(c), pl.ds(land, count)],
+                    push(conc_hbm.at[:, at * halves + h, pl.ds(first, count)],
+                         state0.at[my_gy, :, pl.ds(land, count)],
                          mate(at, h) + (shift if up else -shift),
-                         d_send.at[up, h], a_recv.at[up, c])
+                         d_send.at[up, h], d_recv.at[up])
 
         each_way(act)
 
@@ -160,17 +168,20 @@
                 else:
                     pl.when(cond)(functools.partial(act, o, lv, dev, at))
 
+    send_in(0)
     for_winds(lambda o, lv, dev, at: push(
         wind_hbm.at[:, lv], wrecv.at[at * halves + my_gy], dev, w_send.at[o, lv],
         w_recv.at[at * halves + my_gy]))
     local(wind_hbm.at[:, my_lev], wrecv.at[(seat + 1) * halves + my_gy],
           w_recv.at[(seat + 1) * halves + my_gy])
 
-    @pl.loop(0, chunks)
+    send_own()
+
+    @pl.loop(1, chunks)
     def _(c):
-        pl.when(c < AHEAD)(lambda: send_direct(c))
         send_in(c)
 
+    send_direct()
     def clear(first0, first2):
         @pl.loop(0, halves * chunks)
         def _(i):
@@ -306,10 +317,24 @@
                 state2.at[:, group(c), pl.ds(land, PAD)],
                 me + (shift if up else -shift), b_send.at[up], b_recv.at[up, c]))
 
+    def arrive(up, at):
+        count = reach(at, up)[1]
+        if count > 0:
+            take(state0.at[:, :, pl.ds(0, count)], d_recv.at[up])
+
+    def arrive_relay(c, up, at):
+        total = sum(reach(other, up)[1] for other in range(span) if other != at)
+        if total > 0:
+            take(state0.at[:, group(c), pl.ds(0, total)], a_recv.at[up, c])
+
     def early(c):
-        take(state0.at[:, group(c), pl.ds(0, rows)], in_recv.at[seat, c])
-        pl.when(has_down)(lambda: take(state0.at[:, group(c), pl.ds(0, WIDE)], a_recv.at[1, c]))
-        pl.when(has_up)(lambda: take(state0.at[:, group(c), pl.ds(0, WIDE)], a_recv.at[0, c]))
+
+        @pl.when(c == 0)
+        def _():
+            take(state0.at[:, :, pl.ds(0, rows)], own_recv)
+            each_way(arrive, True)
+
+        each_way(functools.partial(arrive_relay, c), True)
         base = at0(c)
         for q in (0, 1):
             off = passes[q][1]
@@ -386,15 +411,27 @@
                     acc = term if acc is None else acc + term
                 flat_b[pl.ds(base + o * SUB, SUB), :] = acc
 
+    def pass_on(up):
+        pl.semaphore_signal(token.at[up], inc=1, device_id=where_is(me + (shift if up else -shift)),
+                            device_id_type=MESH)
+
+    pl.when(has_up & (crew == 0))(lambda: pass_on(1))
+    pl.when(has_down & (crew == crews - 1))(lambda: pass_on(0))
+
     @pl.loop(0, chunks + LAG_U)
     def _(i):
+        for up, cond, on, turn in ((1, has_down, has_up, crew), (0, has_up, has_down, crews - 1 - crew)):
+            @pl.when(cond & (i == turn))
+            def _():
+                pl.semaphore_wait(token.at[up], 1)
+                pl.when(on)(functools.partial(pass_on, up))
+
         @pl.when(i < chunks)
         def _():
             for k in range(1, span):
                 at = (seat + k) % span
                 take(state0.at[:, group(i), pl.ds(0, rows)], in_recv.at[at, i])
             send_relay(i)
-            pl.when(i + AHEAD < chunks)(lambda: send_direct(i + AHEAD))
 
         @pl.when((i >= LAG_A) & (i < LAG_A + chunks))
         def _():
@@ -470,7 +507,7 @@
     chunk = max(d for d in range(1, WIDTH + 1) if spec % d == 0)
     chunks = spec // chunk
     groups = -(-chunk // SUB)
-    assert chunks * groups <= LANES // 2
+    assert chunks * groups <= LANES // 2 and gx_n // span <= chunks + LAG_B
     deep = span * rows
     dims = (spec, lev, rows, halves, gx_n, span, chunk)
     f32 = jnp.float32
@@ -500,11 +537,11 @@
             pltpu.VMEM((chunks * groups * SUB, lanes), f32),
             dma((3,)),
             dma((3, lev)), dma((slots,)),
-            dma((lev,)), dma((span, chunks)),
-            dma((2, halves)), dma((2,)), dma((2, chunks)),
+            dma((lev,)), dma((span, chunks)), dma(()),
+            dma((2, halves)), dma((2,)), dma((2,)), dma((2, chunks)),
             dma((2,)), dma((2, chunks)),
             dma((lev,)), dma((chunks,)),
-            dma(()), dma(()),
+            dma(()), dma(()), pltpu.SemaphoreType.REGULAR((2,)),
         ],
         compiler_params=pltpu.CompilerParams(collective_id=0, has_side_effects=True),
     )(

time: 28.6 us -> 28.1 us (0.983)
  Pallas kernels: 27.6 us -> 27.2 us
    pallas_call x1, Pallas kernels: 27.6 us -> 27.2 us  [per_device(): pl.pallas_call(functools.partial(kernel, dims), out_shape=pltpu.VMEM((spe...]
where the time goes in v4:
time: 28.1 us; the launch traced here: 28 us
  Pallas kernels  27.2 us (97%)
  local copies, waits for them, and re-layouts  0.8 us (3%)
    pallas_call x1, Pallas kernels, per_device(): pl.pallas_call(functools.partial(kernel, dims), out_shape=pltpu.VMEM((spe...  27.2 us
    unnamed x1, local copies, waits for them, and re-layouts  0.8 us

profile of v4, /device:TPU:0, one launch (start us, length us, event | category | flops | bytes accessed | tf_op | source)
XLA Modules:
  0.0 28.0 jit_solution(16787498410175410736)
XLA Ops:
  0.0 27.2 %shard_map.55 = f32[1056,128]{1,0:T(8,128)S(1)} custom-call(f32[66,4,4,128]{3,2,1,0:T(4,128)} %conc_hbm.1, f32[2,4,4,128]{3,2,1,0:T(4,128)} %wind_hbm.1, f32[3,4,128]{2,1,0:T(4,128)} %diff_hbm.1, f32[264,128]{1,0:T(8,128)} %bitcast.3, f32[66]{0:T(128)} %rate_hbm.1), custom_call_target="tpu_custom_call" | custom-call | tf_op jit(solution)/shard_map/pallas_call | solution.py:517
  27.2 0.8 %copy.7 = f32[66,4,4,128]{3,2,1,0:T(4,128)} copy(f32[66,4,4,128]{3,2,1,0:T(4,128)S(1)} %bitcast.2) | data formatting | bytes 1081344

commit v5 on v4

--- a/solution.py
+++ b/solution.py
@@ -16,6 +16,7 @@
 LAG_B = 10
 LAG_U = 15
 WIDTH = 11
+SLOT = LANES // SUB
 MESH = pl.DeviceIdType.MESH
 
 
@@ -38,7 +39,7 @@
 
 def kernel(dims, conc_hbm, wind_hbm, diff_hbm, emis_hbm, rate_hbm, out_ref,
            rate_ref, diff_ref, emis_ref, state0, state1, state2, result, back,
-           wrecv, cbuf, wts, part, stat, stats, scal,
+           wrecv, cbuf, wts, part, stat, note, stats, scal,
            load_sem, w_send, w_recv, in_send, in_recv, own_recv, d_send, d_recv, r_send, a_recv,
            b_send, b_recv, out_send, out_recv, s_send, s_recv, token):
     spec, lev, rows, halves, gx_n, span, chunk = dims
@@ -384,11 +385,18 @@
         def _():
             def send_stat(k, carry):
                 dev = (k + me) % n
-                push(stat, stats.at[me], dev, s_send, s_recv)
+                push(note, stats.at[me], dev, s_send, s_recv)
                 return carry
 
+            rows_of = []
+            for o in range(2):
+                mine = jnp.where(lane < SLOT, pltpu.roll(acc, o * (LANES // 2), 1), 0.0)
+                spread = pltpu.roll(mine, 0, 1, stride=SLOT, stride_axis=0)
+                rows_of.append(jnp.sum(spread, axis=0, keepdims=True))
+            packed = jnp.concatenate(rows_of, axis=0)
+            note[...] = packed
             lax.fori_loop(1, n, send_stat, 0)
-            stats[pl.ds(me, 1)] = stat[...][None]
+            stats[pl.ds(me, 1)] = packed[None]
 
         for k in range(1, span * halves):
             m = (my_lev + k) % (span * halves)
@@ -470,7 +478,10 @@
     total = stats[0]
     for k in range(1, n):
         total = total + stats[k]
-    quotient = total / pltpu.roll(total, LANES // 2, 1)
+    line = jnp.broadcast_to(total[0:1] / total[1:2], (SUB, LANES))
+    quotient = line
+    for k in range(1, SUB):
+        quotient = jnp.where(sub == k, pltpu.roll(line, LANES - k * SLOT, 1), quotient)
     for c in range(chunks * groups):
         scal[pl.ds(c * SUB, SUB), :] = jnp.broadcast_to(quotient[:, c:c + 1], (SUB, LANES))
 
@@ -507,7 +518,7 @@
     chunk = max(d for d in range(1, WIDTH + 1) if spec % d == 0)
     chunks = spec // chunk
     groups = -(-chunk // SUB)
-    assert chunks * groups <= LANES // 2 and gx_n // span <= chunks + LAG_B
+    assert chunks * groups <= SLOT and gx_n // span <= chunks + LAG_B
     deep = span * rows
     dims = (spec, lev, rows, halves, gx_n, span, chunk)
     f32 = jnp.float32
@@ -533,7 +544,8 @@
             pltpu.VMEM((4, halves, 14, SUB, lanes), f32),
             pltpu.VMEM((2, groups * SUB * SUB, lanes), f32),
             pltpu.VMEM((SUB, lanes), f32),
-            pltpu.VMEM((n, SUB, lanes), f32),
+            pltpu.VMEM((2, lanes), f32),
+            pltpu.VMEM((n, 2, lanes), f32),
             pltpu.VMEM((chunks * groups * SUB, lanes), f32),
             dma((3,)),
             dma((3, lev)), dma((slots,)),

time: 28.1 us -> 27.6 us (0.982)
  Pallas kernels: 27.2 us -> 26.6 us
    pallas_call x1, Pallas kernels: 27.2 us -> 26.6 us  [per_device(): pl.pallas_call(functools.partial(kernel, dims), out_shape=pltpu.VMEM((spe...]
where the time goes in v5:
time: 27.6 us; the launch traced here: 27.4 us
  Pallas kernels  26.6 us (96%)
  local copies, waits for them, and re-layouts  0.8 us (3%)
    pallas_call x1, Pallas kernels, per_device(): pl.pallas_call(functools.partial(kernel, dims), out_shape=pltpu.VMEM((spe...  26.6 us
    unnamed x1, local copies, waits for them, and re-layouts  0.8 us

profile of v5, /device:TPU:0, one launch (start us, length us, event | category | flops | bytes accessed | tf_op | source)
XLA Modules:
  0.0 27.4 jit_solution(4625229064703531215)
XLA Ops:
  0.0 26.6 %shard_map.55 = f32[1056,128]{1,0:T(8,128)S(1)} custom-call(f32[66,4,4,128]{3,2,1,0:T(4,128)} %conc_hbm.1, f32[2,4,4,128]{3,2,1,0:T(4,128)} %wind_hbm.1, f32[3,4,128]{2,1,0:T(4,128)} %diff_hbm.1, f32[264,128]{1,0:T(8,128)} %bitcast.3, f32[66]{0:T(128)} %rate_hbm.1), custom_call_target="tpu_custom_call" | custom-call | tf_op jit(solution)/shard_map/pallas_call | solution.py:528
  26.6 0.8 %copy.7 = f32[66,4,4,128]{3,2,1,0:T(4,128)} copy(f32[66,4,4,128]{3,2,1,0:T(4,128)S(1)} %bitcast.2) | data formatting | bytes 1081344

commit v6 on v5

--- a/solution.py
+++ b/solution.py
@@ -12,9 +12,9 @@
 LANES = 128
 PAD = 3
 WIDE = 2 * PAD
-LAG_A = 5
-LAG_B = 10
-LAG_U = 15
+LAG_A = 6
+LAG_B = 11
+LAG_U = 16
 WIDTH = 11
 SLOT = LANES // SUB
 MESH = pl.DeviceIdType.MESH
@@ -73,8 +73,8 @@
     for cond, move in ((has_down, -shift), (has_up, shift)):
         @pl.when(cond)
         def _():
-            for m in range(lev):
-                greet(mate(m // halves, m % halves) + move)
+            for h in range(halves):
+                greet(mate(seat, h) + move)
 
     loads = [pltpu.make_async_copy(src, dst, load_sem.at[i]) for i, (src, dst) in enumerate(
         ((diff_hbm, diff_ref), (emis_hbm, emis_ref), (rate_hbm, rate_ref)))]
@@ -103,7 +103,7 @@
     zero = jnp.zeros((SUB, LANES), jnp.float32)
     few = jnp.zeros((SUB // 2, LANES), jnp.float32)
 
-    pl.semaphore_wait(barrier, lev - 1 + jnp.where(has_down, lev, 0) + jnp.where(has_up, lev, 0))
+    pl.semaphore_wait(barrier, lev - 1 + jnp.where(has_down, halves, 0) + jnp.where(has_up, halves, 0))
 
     own_rows = pl.ds(SUB + seat * rows, rows)
 
@@ -156,26 +156,38 @@
 
         each_way(act)
 
-    sides = ((0, None, None), (1, has_up & (seat == span - 1), 0),
-             (-1, has_down & (seat == 0), span + 1))
-
-    def for_winds(act):
-        for o, (step, cond, slot) in enumerate(sides):
-            at = seat + 1 if slot is None else slot
-            for lv in range(lev):
-                dev = mate(lv // halves, lv % halves) + step * shift
-                if cond is None:
-                    pl.when(dev != me)(functools.partial(act, o, lv, dev, at))
-                else:
-                    pl.when(cond)(functools.partial(act, o, lv, dev, at))
-
+    edges = ((1, has_up, span - 1, 0), (0, has_down, 0, span + 1))
+
+    def send_winds():
+        for k in range(1, lev):
+            m = (my_lev + k) % lev
+            push(wind_hbm.at[:, m], wrecv.at[(seat + 1) * halves + my_gy], mate(m // halves, m % halves),
+                 w_send.at[2, k], w_recv.at[(seat + 1) * halves + my_gy])
+        local(wind_hbm.at[:, my_lev], wrecv.at[(seat + 1) * halves + my_gy],
+              w_recv.at[(seat + 1) * halves + my_gy])
+        for up, cond, edge, slot in edges:
+            @pl.when(cond & (seat == edge))
+            def _():
+                for h in range(halves):
+                    push(wind_hbm.at[:, edge * halves + h], wrecv.at[slot * halves + my_gy],
+                         mate(edge, h) + (shift if up else -shift),
+                         w_send.at[up, h], w_recv.at[slot * halves + my_gy])
+
+    def relay_winds():
+        for at in range(span):
+            for h in range(halves):
+                k = (at + 1) * halves + h
+                take(wrecv.at[k], w_recv.at[k])
+        for up, cond, edge, slot in edges:
+            @pl.when(cond & (seat != edge))
+            def _():
+                for h in range(halves):
+                    push(wrecv.at[(edge + 1) * halves + h], wrecv.at[slot * halves + h],
+                         me + (shift if up else -shift),
+                         w_send.at[up, h], w_recv.at[slot * halves + h])
+
+    send_winds()
     send_in(0)
-    for_winds(lambda o, lv, dev, at: push(
-        wind_hbm.at[:, lv], wrecv.at[at * halves + my_gy], dev, w_send.at[o, lv],
-        w_recv.at[at * halves + my_gy]))
-    local(wind_hbm.at[:, my_lev], wrecv.at[(seat + 1) * halves + my_gy],
-          w_recv.at[(seat + 1) * halves + my_gy])
-
     send_own()
 
     @pl.loop(1, chunks)
@@ -244,40 +256,45 @@
             for o in range(pairs):
                 out_ref[pl.ds((2 * s + k) * lev * rows + o * SUB, SUB), :] = first_col[o] * v
 
-    def wind_in(slot):
-        for h in range(halves):
-            take(wrecv.at[slot * halves + h], w_recv.at[slot * halves + h])
-            for c in range(2):
-                base = SUB + (slot - 1) * rows
-                cbuf[c, h, base:base + rows, :] = wrecv[slot * halves + h, c]
-
-    for slot in range(1, span + 1):
-        wind_in(slot)
-    pl.when(has_down)(lambda: wind_in(0))
-    pl.when(has_up)(lambda: wind_in(span + 1))
+    relay_winds()
 
     passes = ((0, -PAD), (0, deep - SUB + PAD), (1, 0), (2, 0))
-    for q, (s, r0) in enumerate(passes):
-        at_row = crew * deep + r0 + sub
-        inside = (at_row >= 0) & (at_row < crews * deep)
-        for h in range(halves):
-            here, left, right = (cbuf[0, h, SUB + r0 + d:2 * SUB + r0 + d, :] for d in (0, -1, 1))
-            for j, w in enumerate(stencil_weights(0.5 * (left + here), 0.5 * (here + right))):
-                wts[q, h, j] = jnp.where(inside, w, 0.0) * BETAS[s]
-        cy = [cbuf[1, h, SUB + r0:2 * SUB + r0, :] for h in range(halves)]
-        for h in range(halves):
-            nxt = pltpu.roll(cy[h + 1], LANES - 1, 1) if h + 1 < halves else zero
-            prv = pltpu.roll(cy[h - 1], 1, 1) if h > 0 else zero
-            up = jnp.where(lane < LANES - 1, pltpu.roll(cy[h], LANES - 1, 1), nxt)
-            down = jnp.where(lane >= 1, pltpu.roll(cy[h], 1, 1), prv)
-            ws = stencil_weights(0.5 * (down + cy[h]), 0.5 * (cy[h] + up))
-            for j, w in enumerate(ws):
-                d = j - 3
-                if d > 0 and h == halves - 1:
-                    w = jnp.where(lane < LANES - d, w, 0.0)
-                if d < 0 and h == 0:
-                    w = jnp.where(lane >= -d, w, 0.0)
-                wts[q, h, 7 + j] = w * BETAS[s]
+
+    def weigh():
+        def wind_in(slot, wait=True):
+            for h in range(halves):
+                if wait:
+                    take(wrecv.at[slot * halves + h], w_recv.at[slot * halves + h])
+                for c in range(2):
+                    base = SUB + (slot - 1) * rows
+                    cbuf[c, h, base:base + rows, :] = wrecv[slot * halves + h, c]
+
+        for slot in range(1, span + 1):
+            wind_in(slot, False)
+        pl.when(has_down)(lambda: wind_in(0))
+        pl.when(has_up)(lambda: wind_in(span + 1))
+
+        for q, (s, r0) in enumerate(passes):
+            at_row = crew * deep + r0 + sub
+            inside = (at_row >= 0) & (at_row < crews * deep)
+            for h in range(halves):
+                here, left, right = (cbuf[0, h, SUB + r0 + d:2 * SUB + r0 + d, :] for d in (0, -1, 1))
+                for j, w in enumerate(stencil_weights(0.5 * (left + here), 0.5 * (here + right))):
+                    wts[q, h, j] = jnp.where(inside, w, 0.0) * BETAS[s]
+            cy = [cbuf[1, h, SUB + r0:2 * SUB + r0, :] for h in range(halves)]
+            for h in range(halves):
+                nxt = pltpu.roll(cy[h + 1], LANES - 1, 1) if h + 1 < halves else zero
+                prv = pltpu.roll(cy[h - 1], 1, 1) if h > 0 else zero
+                up = jnp.where(lane < LANES - 1, pltpu.roll(cy[h], LANES - 1, 1), nxt)
+                down = jnp.where(lane >= 1, pltpu.roll(cy[h], 1, 1), prv)
+                ws = stencil_weights(0.5 * (down + cy[h]), 0.5 * (cy[h] + up))
+                for j, w in enumerate(ws):
+                    d = j - 3
+                    if d > 0 and h == halves - 1:
+                        w = jnp.where(lane < LANES - d, w, 0.0)
+                    if d < 0 and h == 0:
+                        w = jnp.where(lane >= -d, w, 0.0)
+                    wts[q, h, 7 + j] = w * BETAS[s]
 
     def step(q, count, src, src_at, start, start_at, put):
         wx = [[wts[q, h, j] for j in range(7)] for h in range(halves)]
@@ -441,6 +458,8 @@
                 take(state0.at[:, group(i), pl.ds(0, rows)], in_recv.at[at, i])
             send_relay(i)
 
+        pl.when(i == LAG_A)(weigh)
+
         @pl.when((i >= LAG_A) & (i < LAG_A + chunks))
         def _():
             early(i - LAG_A)
@@ -453,7 +472,13 @@
         def _():
             solve(i - LAG_U)
 
-    for_winds(lambda o, lv, dev, at: take(wrecv.at[0], w_send.at[o, lv]))
+    for k in range(1, lev):
+        take(wrecv.at[0], w_send.at[2, k])
+    for up, cond, _, _ in edges:
+        @pl.when(cond)
+        def _():
+            for h in range(halves):
+                take(wrecv.at[0], w_send.at[up, h])
     whole = state0.at[0, :, pl.ds(0, rows)]
     for k in range(1, span * halves):
         take(whole, in_send.at[k])

time: 27.6 us -> 26.8 us (0.971)
  Pallas kernels: 26.6 us -> 25.8 us
    pallas_call x1, Pallas kernels: 26.6 us -> 25.8 us  [per_device(): pl.pallas_call(functools.partial(kernel, dims), out_shape=pltpu.VMEM((spe...]
where the time goes in v6:
time: 26.8 us; the launch traced here: 26.7 us
  Pallas kernels  25.8 us (96%)
  local copies, waits for them, and re-layouts  0.8 us (3%)
    pallas_call x1, Pallas kernels, per_device(): pl.pallas_call(functools.partial(kernel, dims), out_shape=pltpu.VMEM((spe...  25.8 us
    unnamed x1, local copies, waits for them, and re-layouts  0.8 us

profile of v6, /device:TPU:0, one launch (start us, length us, event | category | flops | bytes accessed | tf_op | source)
XLA Modules:
  0.0 26.7 jit_solution(4905257497843152180)
XLA Ops:
  0.0 25.8 %shard_map.55 = f32[1056,128]{1,0:T(8,128)S(1)} custom-call(f32[66,4,4,128]{3,2,1,0:T(4,128)} %conc_hbm.1, f32[2,4,4,128]{3,2,1,0:T(4,128)} %wind_hbm.1, f32[3,4,128]{2,1,0:T(4,128)} %diff_hbm.1, f32[264,128]{1,0:T(8,128)} %bitcast.3, f32[66]{0:T(128)} %rate_hbm.1), custom_call_target="tpu_custom_call" | custom-call | tf_op jit(solution)/shard_map/pallas_call | solution.py:553
  25.9 0.8 %copy.7 = f32[66,4,4,128]{3,2,1,0:T(4,128)} copy(f32[66,4,4,128]{3,2,1,0:T(4,128)S(1)} %bitcast.2) | data formatting | bytes 1081344

commit v7 on v6

--- a/solution.py
+++ b/solution.py
@@ -54,27 +54,31 @@
     crew, seat = my_gx // span, my_gx % span
     my_lev = seat * halves + my_gy
     has_down, has_up = crew > 0, crew < crews - 1
-    shift = span * halves
+    here = my_gx, my_gy
 
     def where_is(dev):
-        return {"gx": dev // halves, "gy": dev % halves}
+        return {"gx": dev[0], "gy": dev[1]}
+
+    def beyond(dev, up):
+        return dev[0] + (span if up else -span), dev[1]
 
     def mate(at, half):
-        return (crew * span + at) * halves + half
+        return crew * span + at, half
 
     barrier = pltpu.get_barrier_semaphore()
 
     def greet(dev):
         pl.semaphore_signal(barrier, inc=1, device_id=where_is(dev), device_id_type=MESH)
 
-    for k in range(1, lev):
-        m = (my_lev + k) % lev
-        greet(mate(m // halves, m % halves))
-    for cond, move in ((has_down, -shift), (has_up, shift)):
+    peers = [((seat + k) % span, h) for k in range(1, span) for h in range(halves)]
+    peers += [(seat, (my_gy + k) % halves) for k in range(1, halves)]
+    for at, h in peers:
+        greet(mate(at, h))
+    for cond, up in ((has_up, 1), (has_down, 0)):
         @pl.when(cond)
         def _():
             for h in range(halves):
-                greet(mate(seat, h) + move)
+                greet(beyond(mate(seat, h), up))
 
     loads = [pltpu.make_async_copy(src, dst, load_sem.at[i]) for i, (src, dst) in enumerate(
         ((diff_hbm, diff_ref), (emis_hbm, emis_ref), (rate_hbm, rate_ref)))]
@@ -129,7 +133,7 @@
         return 0, max(0, min(rows, WIDE - at * rows)), SUB + deep + at * rows
 
     def each_way(act, landing=False):
-        for up, cond in ((1, has_down if landing else has_up), (0, has_up if landing else has_down)):
+        for up, cond in ((0, has_up if landing else has_down), (1, has_down if landing else has_up)):
             for at in range(span):
                 pl.when(cond & (seat == at))(functools.partial(act, up, at))
 
@@ -140,7 +144,7 @@
                 for h in range(halves):
                     push(conc_hbm.at[:, at * halves + h, pl.ds(first, count)],
                          state0.at[my_gy, :, pl.ds(land, count)],
-                         mate(at, h) + (shift if up else -shift),
+                         beyond(mate(at, h), up),
                          d_send.at[up, h], d_recv.at[up])
 
         each_way(act)
@@ -152,17 +156,16 @@
                 if other != at and count > 0:
                     push(state0.at[:, group(c), pl.ds(SUB + other * rows + first, count)],
                          state0.at[:, group(c), pl.ds(land, count)],
-                         me + (shift if up else -shift), r_send.at[up], a_recv.at[up, c])
+                         beyond(here, up), r_send.at[up], a_recv.at[up, c])
 
         each_way(act)
 
     edges = ((1, has_up, span - 1, 0), (0, has_down, 0, span + 1))
 
     def send_winds():
-        for k in range(1, lev):
-            m = (my_lev + k) % lev
-            push(wind_hbm.at[:, m], wrecv.at[(seat + 1) * halves + my_gy], mate(m // halves, m % halves),
-                 w_send.at[2, k], w_recv.at[(seat + 1) * halves + my_gy])
+        for k, (at, h) in enumerate(peers):
+            push(wind_hbm.at[:, at * halves + h], wrecv.at[(seat + 1) * halves + my_gy], mate(at, h),
+                 w_send.at[2, k + 1], w_recv.at[(seat + 1) * halves + my_gy])
         local(wind_hbm.at[:, my_lev], wrecv.at[(seat + 1) * halves + my_gy],
               w_recv.at[(seat + 1) * halves + my_gy])
         for up, cond, edge, slot in edges:
@@ -170,7 +173,7 @@
             def _():
                 for h in range(halves):
                     push(wind_hbm.at[:, edge * halves + h], wrecv.at[slot * halves + my_gy],
-                         mate(edge, h) + (shift if up else -shift),
+                         beyond(mate(edge, h), up),
                          w_send.at[up, h], w_recv.at[slot * halves + my_gy])
 
     def relay_winds():
@@ -183,18 +186,18 @@
             def _():
                 for h in range(halves):
                     push(wrecv.at[(edge + 1) * halves + h], wrecv.at[slot * halves + h],
-                         me + (shift if up else -shift),
+                         beyond(here, up),
                          w_send.at[up, h], w_recv.at[slot * halves + h])
 
     send_winds()
     send_in(0)
+    send_direct()
     send_own()
 
     @pl.loop(1, chunks)
     def _(c):
         send_in(c)
 
-    send_direct()
     def clear(first0, first2):
         @pl.loop(0, halves * chunks)
         def _(i):
@@ -333,7 +336,7 @@
             pl.when(cond)(functools.partial(
                 push, state2.at[:, group(c), pl.ds(first, PAD)],
                 state2.at[:, group(c), pl.ds(land, PAD)],
-                me + (shift if up else -shift), b_send.at[up], b_recv.at[up, c]))
+                beyond(here, up), b_send.at[up], b_recv.at[up, c]))
 
     def arrive(up, at):
         count = reach(at, up)[1]
@@ -401,7 +404,8 @@
         @pl.when(c == chunks - 1)
         def _():
             def send_stat(k, carry):
-                dev = (k + me) % n
+                dev = k - 1 + jnp.where(k - 1 >= me, 1, 0)
+                dev = dev // halves, dev % halves
                 push(note, stats.at[me], dev, s_send, s_recv)
                 return carry
 
@@ -415,11 +419,9 @@
             lax.fori_loop(1, n, send_stat, 0)
             stats[pl.ds(me, 1)] = packed[None]
 
-        for k in range(1, span * halves):
-            m = (my_lev + k) % (span * halves)
-            push(result.at[m % halves, group(c), pl.ds((m // halves) * rows, rows)],
-                 back.at[group(c), my_lev], mate(m // halves, m % halves),
-                 out_send.at[k], out_recv.at[c])
+        for k, (at, h) in enumerate(peers):
+            push(result.at[h, group(c), pl.ds(at * rows, rows)],
+                 back.at[group(c), my_lev], mate(at, h), out_send.at[k + 1], out_recv.at[c])
         local(result.at[my_gy, group(c), pl.ds(seat * rows, rows)],
               back.at[group(c), my_lev], out_recv.at[c])
 
@@ -437,7 +439,7 @@
                 flat_b[pl.ds(base + o * SUB, SUB), :] = acc
 
     def pass_on(up):
-        pl.semaphore_signal(token.at[up], inc=1, device_id=where_is(me + (shift if up else -shift)),
+        pl.semaphore_signal(token.at[up], inc=1, device_id=where_is(beyond(here, up)),
                             device_id_type=MESH)
 
     pl.when(has_up & (crew == 0))(lambda: pass_on(1))

time: 26.8 us -> 26.7 us (level)
  no operation moved by 1% of the time
where the time goes in v7:
time: 26.7 us; the launch traced here: 26.6 us
  Pallas kernels  25.8 us (97%)
  local copies, waits for them, and re-layouts  0.8 us (3%)
    pallas_call x1, Pallas kernels, per_device(): pl.pallas_call(functools.partial(kernel, dims), out_shape=pltpu.VMEM((spe...  25.8 us
    unnamed x1, local copies, waits for them, and re-layouts  0.8 us

profile of v7, /device:TPU:0, one launch (start us, length us, event | category | flops | bytes accessed | tf_op | source)
XLA Modules:
  0.0 26.6 jit_solution(13201532594257591124)
XLA Ops:
  0.0 25.8 %shard_map.55 = f32[1056,128]{1,0:T(8,128)S(1)} custom-call(f32[66,4,4,128]{3,2,1,0:T(4,128)} %conc_hbm.1, f32[2,4,4,128]{3,2,1,0:T(4,128)} %wind_hbm.1, f32[3,4,128]{2,1,0:T(4,128)} %diff_hbm.1, f32[264,128]{1,0:T(8,128)} %bitcast.3, f32[66]{0:T(128)} %rate_hbm.1), custom_call_target="tpu_custom_call" | custom-call | tf_op jit(solution)/shard_map/pallas_call | solution.py:555
  25.8 0.8 %copy.7 = f32[66,4,4,128]{3,2,1,0:T(4,128)} copy(f32[66,4,4,128]{3,2,1,0:T(4,128)S(1)} %bitcast.2) | data formatting | bytes 1081344
